TPU v7x, 32 devices: a whole 2x2x4 slice. The times are simulated.
32 devices in a mesh: row: 8 (over y, x, core), col: 4 (over z).
Axes of the slice: x: 2, y: 2, z: 4, core: 2. Of those that a mesh axis runs over, the one named last changes fastest.
Arguments:
- jacobian: float32 [2, 4096, 256], P(None, ('row', 'col')), may hold values from -0.25 to 0.25
Outputs:
- normal_tiles: float32 [8, 2, 4, 512, 512], P('row', None, 'col')
All inputs are finite; a program needn't handle non-finite values.
Results may differ from a plain program's by a relative error of at most 0.0003.
Values sent between devices are 32-bit elements; how exact they have to be, the bound alone decides.
A program may use at most 64 MiB of HBM per device.

v0:
```python
import jax
import jax.numpy as jnp
from jax import lax
from jax.sharding import PartitionSpec as P


def from_partner(block, axis, distance):
    count = lax.axis_size(axis)
    route = []
    for low in range(count):
        high = low | 1 << distance
        if high != low and high < count:
            route += [(low, high), (high, low)]
    return lax.ppermute(block, axis, route)


def partner_rows(block, bit_number):
    return from_partner(block, ("row", "col"), bit_number)


def body(jacobian):
    row_index = lax.axis_index("row")
    col_index = lax.axis_index("col")
    col_count = lax.axis_size("col")
    cycles = lax.axis_size("row") // col_count
    panel_count = jacobian.shape[0]
    width = jacobian.shape[2]
    own_tile = lax.all_gather(jacobian, "col", axis=1, tiled=True)
    tile_size = own_tile.shape[1]
    col_bits = col_count.bit_length() - 1
    low_row = row_index % col_count
    moved = jacobian
    for bit_number in range(col_bits):
        first = partner_rows(moved, bit_number)
        second = partner_rows(first, bit_number + col_bits)
        differ = low_row >> bit_number & 1 != col_index >> bit_number & 1
        moved = jnp.where(differ, second, moved)
    gathered = lax.all_gather(moved, "row", axis=1, tiled=True)
    gathered = gathered.reshape(panel_count, cycles, tile_size, width)
    partners = [gathered[:, turn_index] for turn_index in range(cycles)]

    def product(partner):
        return jnp.einsum("pak,pbk->ab", own_tile, partner, precision=lax.Precision.HIGHEST)

    def empty_tile(partner):
        return jnp.zeros((tile_size, tile_size), jnp.float32)

    results = []
    for turn_index in range(cycles):
        column_tile = col_index + col_count * turn_index
        results.append(
            lax.cond(column_tile <= row_index, product, empty_tile, partners[turn_index])
        )
    blocks = jnp.stack(results, 0)
    return blocks[None, :, None]


def solution(mesh):
    in_specs = (P(None, ("row", "col"), None),)
    out_specs = P("row", None, "col", None, None)
    return jax.shard_map(body, mesh=mesh, in_specs=in_specs, out_specs=out_specs, check_vma=False)
```

profile of v0, /device:TPU:4, one launch (start us, length us, event | category | flops | bytes accessed | tf_op | source)
XLA Modules:
  0.0 115.7 jit_solution(6772489944896085306)
XLA Ops:
  6.5 0.0 all-gather.3.cloned.1.call-start
  6.5 1.6 %collective-permute-start = (f32[2,128,256]{2,1,0:T(8,128)}, f32[2,128,256]{2,1,0:T(8,128)S(1)}, u32[]{:S(2)}, u32[]{:S(2)}) collective-permute-start(f32[2,128,256]{2,1,0:T(8,128)} %param.5), channel_id=1, source_target_pairs={{0,1},{1,0},{2,3},{3,2},{4,5},{5,4},{6,7},{7,6},{8,9},{9,8},{10,11... | collective-permute-start | bytes 786440 | tf_op jit(solution)/shard_map/ppermute | solution.py:14
  8.1 6.7 %collective-permute-done = f32[2,128,256]{2,1,0:T(8,128)S(1)} collective-permute-done((f32[2,128,256]{2,1,0:T(8,128)}, f32[2,128,256]{2,1,0:T(8,128)S(1)}, u32[]{:S(2)}, u32[]{:S(2)}) %collective-permute-start) | collective-permute-done | bytes 262176 | tf_op jit(solution)/shard_map/ppermute | solution.py:14
  14.8 0.0 collective-permute-start.1
  14.8 1.5 %collective-permute-done.1 = f32[2,128,256]{2,1,0:T(8,128)S(1)} collective-permute-done((f32[2,128,256]{2,1,0:T(8,128)S(1)}, f32[2,128,256]{2,1,0:T(8,128)S(1)}, u32[]{:S(2)}, u32[]{:S(2)}) %collective-permute-start.1) | collective-permute-done | bytes 262176 | tf_op jit(solution)/shard_map/ppermute | solution.py:14
  16.3 1.0 broadcast_select_fusion
  17.3 2.7 %collective-permute-start.2 = (f32[2,128,256]{2,1,0:T(8,128)S(1)}, f32[2,128,256]{2,1,0:T(8,128)S(1)}, u32[]{:S(2)}, u32[]{:S(2)}) collective-permute-start(f32[2,128,256]{2,1,0:T(8,128)S(1)} %broadcast_select_fusion), channel_id=1, source_target_pairs={{0,2},{2,0},{1,3},{3,1},{4,6},{6,4},{5,7},{7,5},{8,10},{10,8},{9,1... | collective-permute-start | bytes 786440 | tf_op jit(solution)/shard_map/ppermute | solution.py:14
  20.0 11.3 %collective-permute-done.2 = f32[2,128,256]{2,1,0:T(8,128)S(1)} collective-permute-done((f32[2,128,256]{2,1,0:T(8,128)S(1)}, f32[2,128,256]{2,1,0:T(8,128)S(1)}, u32[]{:S(2)}, u32[]{:S(2)}) %collective-permute-start.2) | collective-permute-done | bytes 262176 | tf_op jit(solution)/shard_map/ppermute | solution.py:14
  31.3 1.5 %collective-permute-start.3 = (f32[2,128,256]{2,1,0:T(8,128)S(1)}, f32[2,128,256]{2,1,0:T(8,128)S(1)}, u32[]{:S(2)}, u32[]{:S(2)}) collective-permute-start(f32[2,128,256]{2,1,0:T(8,128)S(1)} %collective-permute-done.2), channel_id=1, source_target_pairs={{0,8},{8,0},{1,9},{9,1},{2,10},{10,2},{3,11},{11,3},{4,12},{12,4},... | collective-permute-start | bytes 786440 | tf_op jit(solution)/shard_map/ppermute | solution.py:14
  32.8 5.1 %collective-permute-done.3 = f32[2,128,256]{2,1,0:T(8,128)S(1)} collective-permute-done((f32[2,128,256]{2,1,0:T(8,128)S(1)}, f32[2,128,256]{2,1,0:T(8,128)S(1)}, u32[]{:S(2)}, u32[]{:S(2)}) %collective-permute-start.3) | collective-permute-done | bytes 262176 | tf_op jit(solution)/shard_map/ppermute | solution.py:14
  37.8 0.7 broadcast_select_fusion.1
  38.6 0.0 all-gather.3.cloned.1.call-update
  38.6 0.0 all-gather.5.cloned.1.call-start
  38.7 0.7 all-gather.5.cloned.1.call-update
  39.4 30.0 %all-gather.3.cloned.1.call-done = f32[2,1024,256]{2,1,0:T(8,128)} async-done(((f32[2,128,256]{2,1,0:T(8,128)}), f32[2,1024,256]{2,1,0:T(8,128)}) %all-gather.3.cloned.1.call-update) | async-done | bytes 2097168 | tf_op jit(solution)/shard_map/all_gather | solution.py:38
  69.3 1.7 %copy.2 = f32[2,2,512,256]{3,2,0,1:T(8,128)S(1)} copy(f32[2,2,512,256]{3,2,1,0:T(8,128)} %bitcast.17) | data formatting | bytes 4194304 | tf_op jit(solution)/shard_map/cond | solution.py:52
  71.1 27.9 %all-gather.5.cloned.1.call-done = f32[2,512,256]{2,1,0:T(8,128)} async-done(((f32[2,128,256]{2,1,0:T(8,128)}), f32[2,512,256]{2,1,0:T(8,128)}) %all-gather.5.cloned.1.call-update) | async-done | bytes 1048592 | tf_op jit(solution)/shard_map/all_gather | solution.py:28
  99.0 3.1 %conditional.3 = (f32[1,512,512]{2,1,0:T(8,128)S(1)}) conditional(s32[]{:T(128)} %convert_element_type.7, () %tuple.23, (f32[2,2,512,256]{3,2,0,1:T(8,128)S(1)}, f32[2,512,256]{2,1,0:T(8,128)}) %tuple.24), branch_computations={%region_2.3_spmd, %region_3.4_spmd} | conditional | flops 1610612736 | bytes 3145736 | solution.py:52
  99.0 3.1 %convolution_bitcast_fusion.1 = f32[1,512,512]{2,1,0:T(8,128)S(1)} fusion(f32[2,512,256]{2,1,0:T(8,128)} %get-tuple-element.27, f32[2,2,512,256]{3,2,0,1:T(8,128)S(1)} %get-tuple-element.28), kind=kOutput, calls=%fused_computation.3 | convolution fusion | flops 1610612736 | bytes 3145728 | tf_op jit(solution)/shard_map/cond/branch_1_fun/pak,pbk->ab/dot_general | solution.py:43
  102.1 4.1 %conditional.2 = (f32[1,512,512]{2,1,0:T(8,128)}) conditional(s32[]{:T(128)} %convert_element_type.6, () %tuple.21, (f32[2,2,512,256]{3,2,0,1:T(8,128)S(1)}, f32[2,512,256]{2,1,0:T(8,128)}) %tuple.24), branch_computations={%region_0.1_spmd, %region_1.2_spmd} | conditional | flops 1610612736 | bytes 3145736 | solution.py:52
  102.1 4.1 %convolution_bitcast_fusion = f32[1,512,512]{2,1,0:T(8,128)} fusion(f32[2,512,256]{2,1,0:T(8,128)} %get-tuple-element.25, f32[2,2,512,256]{3,2,0,1:T(8,128)S(1)} %get-tuple-element.26), kind=kOutput, calls=%fused_computation | convolution fusion | flops 1610612736 | bytes 3145728 | tf_op jit(solution)/shard_map/cond/branch_1_fun/pak,pbk->ab/dot_general | solution.py:43
  106.2 2.7 %maximum_bitcast_fusion = f32[1,2,1,512,512]{4,3,2,1,0:T(8,128)} fusion(f32[1,512,512]{2,1,0:T(8,128)S(1)} %get-tuple-element.34, f32[1,512,512]{2,1,0:T(8,128)} %get-tuple-element.33), kind=kLoop, calls=%fused_computation.6 | loop fusion | flops 524288 | bytes 4194304 | tf_op jit(solution)/shard_map/broadcast_in_dim | solution.py:55
Async XLA Ops:
  6.5 62.8 %all-gather.3.cloned.1.call-start = ((), (), s32[]{:S(2)}) async-start(), calls=%async_computation | async-start | bytes 2359296 | tf_op jit(solution)/shard_map/all_gather | solution.py:38
  6.5 8.3 %collective-permute-start = (f32[2,128,256]{2,1,0:T(8,128)}, f32[2,128,256]{2,1,0:T(8,128)S(1)}, u32[]{:S(2)}, u32[]{:S(2)}) collective-permute-start(f32[2,128,256]{2,1,0:T(8,128)} %param.5), channel_id=1, source_target_pairs={{0,1},{1,0},{2,3},{3,2},{4,5},{5,4},{6,7},{7,6},{8,9},{9,8},{10,11... | collective-permute-start | bytes 786440 | tf_op jit(solution)/shard_map/ppermute | solution.py:14
  14.8 1.5 %collective-permute-start.1 = (f32[2,128,256]{2,1,0:T(8,128)S(1)}, f32[2,128,256]{2,1,0:T(8,128)S(1)}, u32[]{:S(2)}, u32[]{:S(2)}) collective-permute-start(f32[2,128,256]{2,1,0:T(8,128)S(1)} %collective-permute-done), channel_id=1, source_target_pairs={{0,4},{4,0},{1,5},{5,1},{2,6},{6,2},{3,7},{7,3},{8,12},{12,8},{9,1... | collective-permute-start | bytes 786440 | tf_op jit(solution)/shard_map/ppermute | solution.py:14
  17.3 14.0 %collective-permute-start.2 = (f32[2,128,256]{2,1,0:T(8,128)S(1)}, f32[2,128,256]{2,1,0:T(8,128)S(1)}, u32[]{:S(2)}, u32[]{:S(2)}) collective-permute-start(f32[2,128,256]{2,1,0:T(8,128)S(1)} %broadcast_select_fusion), channel_id=1, source_target_pairs={{0,2},{2,0},{1,3},{3,1},{4,6},{6,4},{5,7},{7,5},{8,10},{10,8},{9,1... | collective-permute-start | bytes 786440 | tf_op jit(solution)/shard_map/ppermute | solution.py:14
  31.3 6.5 %collective-permute-start.3 = (f32[2,128,256]{2,1,0:T(8,128)S(1)}, f32[2,128,256]{2,1,0:T(8,128)S(1)}, u32[]{:S(2)}, u32[]{:S(2)}) collective-permute-start(f32[2,128,256]{2,1,0:T(8,128)S(1)} %collective-permute-done.2), channel_id=1, source_target_pairs={{0,8},{8,0},{1,9},{9,1},{2,10},{10,2},{3,11},{11,3},{4,12},{12,4},... | collective-permute-start | bytes 786440 | tf_op jit(solution)/shard_map/ppermute | solution.py:14
  38.6 60.4 %all-gather.5.cloned.1.call-start = ((), (), s32[]{:S(2)}) async-start(), calls=%async_computation.1 | async-start | bytes 1310720 | tf_op jit(solution)/shard_map/all_gather | solution.py:28
Sparse Core Ops, SparseCore 0:
  38.7 30.5 all-gather.2
  70.9 28.0 all-gather.4
where the time goes:
time: 116 us
  waiting for transfers between devices  83.2 us (72%)
  between operations  13.4 us (12%)
  matrix products  7.14 us (6%)
  starting transfers between devices  5.77 us (5%)
  other arithmetic  4.43 us (4%)
  local copies, waits for them, and re-layouts  1.73 us (1%)
    all_gather x1, waiting for transfers between devices, body(): gathered = lax.all_gather(moved, 'row', axis=1, tiled=True)  30 us
    all_gather x1, waiting for transfers between devices, body(): own_tile = lax.all_gather(jacobian, 'col', axis=1, tiled=True)  27.9 us
    ppermute x4, waiting for transfers between devices, from_partner(): return lax.ppermute(block, axis, route)  24.6 us
    dot_general x2, matrix products, product(): jnp.einsum('pak,pbk->ab', own_tile, partner, precision=lax.Precision.HIGH...  7.14 us
    ppermute x4, starting transfers between devices, from_partner(): return lax.ppermute(block, axis, route)  5.72 us
    broadcast_in_dim x1, other arithmetic, body(): return blocks[None, :, None]  2.71 us
  transfers between devices with their start and end apart: 6, of which 6 were waited for; matrix products, arithmetic and copies ran while one was open for 1% of the time, Pallas kernels for 0%

commit v1 on v0

--- a/solution.py
+++ b/solution.py
@@ -25,7 +25,7 @@
     cycles = lax.axis_size("row") // col_count
     panel_count = jacobian.shape[0]
     width = jacobian.shape[2]
-    own_tile = lax.all_gather(jacobian, "col", axis=1, tiled=True)
+    own_tile = jnp.concatenate(lax.all_gather(jacobian, axis_name="col"), 1)
     tile_size = own_tile.shape[1]
     col_bits = col_count.bit_length() - 1
     low_row = row_index % col_count

time: 116 us -> 97.8 us (0.84)
  waiting for transfers between devices: 83.2 us -> 67.2 us
  other arithmetic: 4.43 us -> 3.22 us
    all_gather x1, waiting for transfers between devices: 27.9 us -> 0.02 us  [body(): own_tile = jnp.concatenate(lax.all_gather(jacobian, axis_name='col'), 1)]
    ppermute x4, waiting for transfers between devices: 24.6 us -> 39 us  [from_partner(): return lax.ppermute(block, axis, route)]
    all_gather x1, waiting for transfers between devices: 30 us -> 27.5 us  [body(): gathered = lax.all_gather(moved, 'row', axis=1, tiled=True)]
    cond x1 -> x0, local copies, waits for them, and re-layouts: 1.73 us -> none  [body(): lax.cond(column_tile <= row_index, product, empty_tile, partners[turn_ind...]
    reshape x0 -> x1, local copies, waits for them, and re-layouts: none -> 1.33 us  [body(): own_tile = jnp.concatenate(lax.all_gather(jacobian, axis_name='col'), 1)]
    broadcast_in_dim x1, other arithmetic: 2.71 us -> 1.49 us  [body(): return blocks[None, :, None]]
  transfers between devices with their start and end apart: 6 -> 6, of which waited for: 6 -> 5; matrix products, arithmetic and copies ran while one was open for 1% -> 3% of each run, Pallas kernels for 0% -> 0%
where the time goes in v1:
time: 97.8 us; the launch traced here: 97.2 us
  waiting for transfers between devices  67.2 us (69%)
  between operations  13.4 us (14%)
  matrix products  6.16 us (6%)
  starting transfers between devices  5.84 us (6%)
  other arithmetic  3.22 us (3%)
  local copies, waits for them, and re-layouts  1.33 us (1%)
    ppermute x4, waiting for transfers between devices, from_partner(): return lax.ppermute(block, axis, route)  39 us
    all_gather x1, waiting for transfers between devices, body(): gathered = lax.all_gather(moved, 'row', axis=1, tiled=True)  27.5 us
    dot_general x2, matrix products, product(): jnp.einsum('pak,pbk->ab', own_tile, partner, precision=lax.Precision.HIGH...  6.16 us
    ppermute x4, starting transfers between devices, from_partner(): return lax.ppermute(block, axis, route)  5.8 us
  transfers between devices with their start and end apart: 6, of which 5 were waited for; matrix products, arithmetic and copies ran while one was open for 3% of the time, Pallas kernels for 0%

profile of v1, /device:TPU:4, one launch (start us, length us, event | category | flops | bytes accessed | tf_op | source)
XLA Modules:
  0.0 97.2 jit_solution(4668967928208689086)
XLA Ops:
  6.5 0.0 all-gather.6.cloned.1.call-start
  6.5 0.7 all-gather.6.cloned.1.call-update
  7.3 0.0 all-gather.4.cloned.1.call-start
  7.3 1.6 %collective-permute-start = (f32[2,128,256]{2,1,0:T(8,128)}, f32[2,128,256]{2,1,0:T(8,128)S(1)}, u32[]{:S(2)}, u32[]{:S(2)}) collective-permute-start(f32[2,128,256]{2,1,0:T(8,128)} %param.5), channel_id=1, source_target_pairs={{0,1},{1,0},{2,3},{3,2},{4,5},{5,4},{6,7},{7,6},{8,9},{9,8},{10,11... | collective-permute-start | bytes 786440 | tf_op jit(solution)/shard_map/ppermute | solution.py:14
  8.9 6.7 %collective-permute-done = f32[2,128,256]{2,1,0:T(8,128)S(1)} collective-permute-done((f32[2,128,256]{2,1,0:T(8,128)}, f32[2,128,256]{2,1,0:T(8,128)S(1)}, u32[]{:S(2)}, u32[]{:S(2)}) %collective-permute-start) | collective-permute-done | bytes 262176 | tf_op jit(solution)/shard_map/ppermute | solution.py:14
  15.6 0.0 collective-permute-start.1
  15.6 1.5 %collective-permute-done.1 = f32[2,128,256]{2,1,0:T(8,128)S(1)} collective-permute-done((f32[2,128,256]{2,1,0:T(8,128)S(1)}, f32[2,128,256]{2,1,0:T(8,128)S(1)}, u32[]{:S(2)}, u32[]{:S(2)}) %collective-permute-start.1) | collective-permute-done | bytes 262176 | tf_op jit(solution)/shard_map/ppermute | solution.py:14
  17.2 1.0 %broadcast_select_fusion = f32[2,128,256]{2,1,0:T(8,128)S(1)} fusion(f32[2,128,256]{2,1,0:T(8,128)S(1)} %collective-permute-done.1, f32[2,128,256]{2,1,0:T(8,128)} %param.5, pred[]{:T(512)S(6)} %ne.14), kind=kLoop, calls=%fused_computation.5 | loop fusion | flops 65536 | bytes 786433 | tf_op jit(solution)/shard_map/jit(_where)/select_n | solution.py:37
  18.2 2.7 %collective-permute-start.2 = (f32[2,128,256]{2,1,0:T(8,128)S(1)}, f32[2,128,256]{2,1,0:T(8,128)S(1)}, u32[]{:S(2)}, u32[]{:S(2)}) collective-permute-start(f32[2,128,256]{2,1,0:T(8,128)S(1)} %broadcast_select_fusion), channel_id=1, source_target_pairs={{0,2},{2,0},{1,3},{3,1},{4,6},{6,4},{5,7},{7,5},{8,10},{10,8},{9,1... | collective-permute-start | bytes 786440 | tf_op jit(solution)/shard_map/ppermute | solution.py:14
  20.8 25.9 %collective-permute-done.2 = f32[2,128,256]{2,1,0:T(8,128)S(1)} collective-permute-done((f32[2,128,256]{2,1,0:T(8,128)S(1)}, f32[2,128,256]{2,1,0:T(8,128)S(1)}, u32[]{:S(2)}, u32[]{:S(2)}) %collective-permute-start.2) | collective-permute-done | bytes 262176 | tf_op jit(solution)/shard_map/ppermute | solution.py:14
  46.7 1.5 %collective-permute-start.3 = (f32[2,128,256]{2,1,0:T(8,128)S(1)}, f32[2,128,256]{2,1,0:T(8,128)S(1)}, u32[]{:S(2)}, u32[]{:S(2)}) collective-permute-start(f32[2,128,256]{2,1,0:T(8,128)S(1)} %collective-permute-done.2), channel_id=1, source_target_pairs={{0,8},{8,0},{1,9},{9,1},{2,10},{10,2},{3,11},{11,3},{4,12},{12,4},... | collective-permute-start | bytes 786440 | tf_op jit(solution)/shard_map/ppermute | solution.py:14
  48.2 4.9 %collective-permute-done.3 = f32[2,128,256]{2,1,0:T(8,128)S(1)} collective-permute-done((f32[2,128,256]{2,1,0:T(8,128)S(1)}, f32[2,128,256]{2,1,0:T(8,128)S(1)}, u32[]{:S(2)}, u32[]{:S(2)}) %collective-permute-start.3) | collective-permute-done | bytes 262176 | tf_op jit(solution)/shard_map/ppermute | solution.py:14
  53.1 0.7 broadcast_select_fusion.1
  53.8 0.0 all-gather.4.cloned.1.call-update
  53.8 0.0 all-gather.6.cloned.1.call-done
  53.9 1.3 %copy.6 = f32[2,4,128,256]{3,2,1,0:T(8,128)S(1)} copy(f32[2,4,128,256]{3,2,0,1:T(8,128)} %bitcast.25) | data formatting | bytes 2097152 | tf_op jit(solution)/shard_map/reshape | solution.py:28
  55.2 27.5 %all-gather.4.cloned.1.call-done = f32[2,1024,256]{2,1,0:T(8,128)} async-done(((f32[2,128,256]{2,1,0:T(8,128)}), f32[2,1024,256]{2,1,0:T(8,128)}) %all-gather.4.cloned.1.call-update) | async-done | bytes 2097168 | tf_op jit(solution)/shard_map/all_gather | solution.py:38
  82.7 3.1 %conditional.3 = (f32[1,512,512]{2,1,0:T(8,128)S(1)}) conditional(s32[]{:T(128)} %convert_element_type.7, () %tuple.23, (f32[2,2,512,256]{3,2,1,0:T(8,128)}, f32[2,512,256]{2,1,0:T(8,128)S(1)}) %tuple.38), branch_computations={%region_2.3_spmd, %region_3.4_spmd} | conditional | flops 1610612736 | bytes 3145736 | solution.py:52
  82.7 3.1 %convolution_bitcast_fusion.1 = f32[1,512,512]{2,1,0:T(8,128)S(1)} fusion(f32[2,512,256]{2,1,0:T(8,128)S(1)} %get-tuple-element.27, f32[2,2,512,256]{3,2,1,0:T(8,128)} %get-tuple-element.35), kind=kOutput, calls=%fused_computation.2 | convolution fusion | flops 1610612736 | bytes 3145728 | tf_op jit(solution)/shard_map/cond/branch_1_fun/pak,pbk->ab/dot_general | solution.py:43
  85.8 3.1 %conditional.2 = (f32[1,512,512]{2,1,0:T(8,128)S(1)}) conditional(s32[]{:T(128)} %convert_element_type.6, () %tuple.21, (f32[2,2,512,256]{3,2,1,0:T(8,128)}, f32[2,512,256]{2,1,0:T(8,128)S(1)}) %tuple.39), branch_computations={%region_0.1_spmd, %region_1.2_spmd} | conditional | flops 1610612736 | bytes 3145736 | solution.py:52
  85.8 3.1 %convolution_bitcast_fusion = f32[1,512,512]{2,1,0:T(8,128)S(1)} fusion(f32[2,512,256]{2,1,0:T(8,128)S(1)} %get-tuple-element.25, f32[2,2,512,256]{3,2,1,0:T(8,128)} %get-tuple-element.33), kind=kOutput, calls=%fused_computation | convolution fusion | flops 1610612736 | bytes 3145728 | tf_op jit(solution)/shard_map/cond/branch_1_fun/pak,pbk->ab/dot_general | solution.py:43
  88.9 1.5 %maximum_bitcast_fusion = f32[1,2,1,512,512]{4,3,2,1,0:T(8,128)} fusion(f32[1,512,512]{2,1,0:T(8,128)S(1)} %get-tuple-element.38, f32[1,512,512]{2,1,0:T(8,128)S(1)} %get-tuple-element.37), kind=kLoop, calls=%fused_computation.4 | loop fusion | flops 524288 | bytes 4194304 | tf_op jit(solution)/shard_map/broadcast_in_dim | solution.py:55
Async XLA Ops:
  6.5 47.3 %all-gather.6.cloned.1.call-start = ((), (), s32[]{:S(2)}) async-start(), calls=%async_computation.1 | async-start | bytes 1310720 | tf_op jit(solution)/shard_map/all_gather | solution.py:28
  7.3 75.4 %all-gather.4.cloned.1.call-start = ((), (), s32[]{:S(2)}) async-start(), calls=%async_computation | async-start | bytes 2359296 | tf_op jit(solution)/shard_map/all_gather | solution.py:38
  7.3 8.3 %collective-permute-start = (f32[2,128,256]{2,1,0:T(8,128)}, f32[2,128,256]{2,1,0:T(8,128)S(1)}, u32[]{:S(2)}, u32[]{:S(2)}) collective-permute-start(f32[2,128,256]{2,1,0:T(8,128)} %param.5), channel_id=1, source_target_pairs={{0,1},{1,0},{2,3},{3,2},{4,5},{5,4},{6,7},{7,6},{8,9},{9,8},{10,11... | collective-permute-start | bytes 786440 | tf_op jit(solution)/shard_map/ppermute | solution.py:14
  15.6 1.5 %collective-permute-start.1 = (f32[2,128,256]{2,1,0:T(8,128)S(1)}, f32[2,128,256]{2,1,0:T(8,128)S(1)}, u32[]{:S(2)}, u32[]{:S(2)}) collective-permute-start(f32[2,128,256]{2,1,0:T(8,128)S(1)} %collective-permute-done), channel_id=1, source_target_pairs={{0,4},{4,0},{1,5},{5,1},{2,6},{6,2},{3,7},{7,3},{8,12},{12,8},{9,1... | collective-permute-start | bytes 786440 | tf_op jit(solution)/shard_map/ppermute | solution.py:14
  18.2 28.5 %collective-permute-start.2 = (f32[2,128,256]{2,1,0:T(8,128)S(1)}, f32[2,128,256]{2,1,0:T(8,128)S(1)}, u32[]{:S(2)}, u32[]{:S(2)}) collective-permute-start(f32[2,128,256]{2,1,0:T(8,128)S(1)} %broadcast_select_fusion), channel_id=1, source_target_pairs={{0,2},{2,0},{1,3},{3,1},{4,6},{6,4},{5,7},{7,5},{8,10},{10,8},{9,1... | collective-permute-start | bytes 786440 | tf_op jit(solution)/shard_map/ppermute | solution.py:14
  46.7 6.4 %collective-permute-start.3 = (f32[2,128,256]{2,1,0:T(8,128)S(1)}, f32[2,128,256]{2,1,0:T(8,128)S(1)}, u32[]{:S(2)}, u32[]{:S(2)}) collective-permute-start(f32[2,128,256]{2,1,0:T(8,128)S(1)} %collective-permute-done.2), channel_id=1, source_target_pairs={{0,8},{8,0},{1,9},{9,1},{2,10},{10,2},{3,11},{11,3},{4,12},{12,4},... | collective-permute-start | bytes 786440 | tf_op jit(solution)/shard_map/ppermute | solution.py:14
Sparse Core Ops, SparseCore 0:
  8.9 40.4 all-gather.5
  53.9 28.7 all-gather.3
